TPU v7x, 128 devices: a whole 4x4x4 slice. The times are simulated.
128 devices in a mesh: rows: 32 (over z, y, core), sub: 4 (over x).
Axes of the slice: x: 4, y: 4, z: 4, core: 2. Of those that a mesh axis runs over, the one named last changes fastest.
Arguments:
- snapshots: float32 [513, 131072], P(None, ('rows', 'sub')), may hold values from -6 to 6
- start: float32 [512, 64], replicated, may hold values from -6 to 6
Outputs:
- modes: float32 [128, 131072], P(None, ('rows', 'sub'))
- operator: float32 [128, 128], replicated
- coefficients: float32 [128, 513], replicated
All inputs are finite; a program needn't handle non-finite values.
Results may differ from a plain program's by a relative error of at most 0.0003.
Values sent between devices are 32-bit elements; how exact they have to be, the bound alone decides.
A program may use at most 64 MiB of HBM per device.

v0:
```python
import jax
import jax.numpy as jnp
from jax import lax
from jax.experimental import pallas as pl
from jax.experimental.pallas import tpu as pltpu
from jax.sharding import Mesh
from jax.sharding import PartitionSpec as P

ROWS_SUB = ("rows_0", "rows_1", "rows_2", "sub")
F32 = jnp.float32
BF16 = jnp.bfloat16
MESH = pl.DeviceIdType.MESH
HI = lax.Precision.HIGHEST
W = 64
PAST = 512
CELLS_HERE = 1024
BLOCKS = [(0, 0), (0, 1), (0, 2), (0, 3), (1, 1), (1, 2), (1, 3), (2, 2), (2, 3), (3, 3)]
TILES = 16 * len(BLOCKS)
HALF = TILES // 2
PIECE = HALF // 16


def dot_nn(a, b, precision=HI):
    return lax.dot_general(a, b, (((1,), (0,)), ((), ())), precision=precision, preferred_element_type=F32)


def dot_nt(a, b, precision=HI):
    return lax.dot_general(a, b, (((1,), (1,)), ((), ())), precision=precision, preferred_element_type=F32)


def dot_tn(a, b, precision=HI):
    return lax.dot_general(a, b, (((0,), (0,)), ((), ())), precision=precision, preferred_element_type=F32)


def iota(shape, dim):
    return lax.broadcasted_iota(jnp.int32, shape, dim)


def eliminate(mats):
    sub = iota((8, 128), 0)
    works = []
    eye = jnp.where(iota((W, W), 0) == iota((W, W), 1), 1.0, 0.0).astype(F32)
    for s in mats:
        aug = jnp.concatenate([s, eye], 1)
        works.append([aug[8 * i : 8 * i + 8] for i in range(8)])
    for k in range(8):
        for v in works:
            col = {}
            for i in range(k, 8):
                for q in range(8):
                    at = 8 * k + q
                    col[i, q] = jnp.broadcast_to(v[i][:, at : at + 1], (8, 128))
            scale = jnp.ones((8, 128), F32)
            for q in range(8):
                pivot = jnp.broadcast_to(col[k, q][q : q + 1], (8, 128))
                inv = lax.rsqrt(pivot)
                scale = jnp.where(sub == q, inv, scale)
                row = jnp.broadcast_to(v[k][q : q + 1], (8, 128)) * inv
                own = jnp.where(sub > q, col[k, q] * inv, 0.0)
                v[k] = v[k] - own * row
                low = {i: col[i, q] * inv for i in range(k + 1, 8)}
                for p in range(q + 1, 8):
                    at = jnp.broadcast_to(own[p : p + 1], (8, 128))
                    col[k, p] = col[k, p] - own * at
                    for i in low:
                        col[i, p] = col[i, p] - low[i] * at
                for i in low:
                    v[i] = v[i] - low[i] * row
            v[k] = v[k] * scale
    keep = iota((W, 128), 1) >= iota((W, 128), 0)
    return [jnp.where(keep, jnp.concatenate(v, 0), 0.0) for v in works]


def apply_u(fac, z):
    return dot_nn(fac, jnp.concatenate([z, jnp.zeros_like(z)], 0))


def apply_x(fac, z):
    return dot_nn(fac, jnp.concatenate([jnp.zeros_like(z), z], 0))


def apply_xt(fac, z):
    return dot_tn(fac, z)[W:]


def orth_kernel(start_ref, out_ref):
    start = start_ref[...]
    st = jnp.concatenate([start, jnp.zeros_like(start)], 1).T[:W]
    fac = eliminate([dot_nt(st, st)])[0]
    out_ref[...] = apply_x(fac, st)


def ring(axis, step):
    n = lax.axis_size(axis)
    return lax.rem(lax.axis_index(axis) + (step + n) % n, n)


def gram_kernel(x_ref, out_ref, hi, lo, part, mine, recv0, buf_a, buf_b, s0, r0, sa, ra, sb, rb, sg, rg, sd, rd):
    z, y, c, x = (lax.axis_index(a) for a in ROWS_SUB)
    offsets = [(o // 4, o % 4) for o in range(16)]

    def plane(o):
        return {"rows_1": ring("rows_1", offsets[o][0]), "sub": ring("sub", offsets[o][1])}

    def plane_source(o):
        return ring("rows_1", -offsets[o][0]) * 4 + ring("sub", -offsets[o][1])

    def plane_target(o):
        return ring("rows_1", offsets[o][0]) * 4 + ring("sub", offsets[o][1])

    barrier = pltpu.get_barrier_semaphore()
    partner = {"rows_2": 1 - c}
    pl.semaphore_signal(barrier, inc=1, device_id=partner, device_id_type=MESH)
    for o in range(1, 16):
        pl.semaphore_signal(barrier, inc=1, device_id=plane(o), device_id_type=MESH)
    for dz in range(1, 4):
        pl.semaphore_signal(barrier, inc=1, device_id={"rows_0": ring("rows_0", dz)}, device_id_type=MESH)

    last = jnp.broadcast_to(x_ref[PAST : PAST + 1], (16, CELLS_HERE))
    hl = last.astype(BF16)
    hi[0:16] = hl
    lo[0:16] = (last - hl.astype(F32)).astype(BF16)
    for r in range(0, PAST, 128):
        v = x_ref[r : r + 128]
        h = v.astype(BF16)
        hi[16 + r : 144 + r] = h
        lo[16 + r : 144 + r] = (v - h.astype(F32)).astype(BF16)
    lane = iota((8, 128), 1)
    row = iota((8, 128), 0)
    at = 0
    g = None
    for s in range(4):
        top = 0 if s == 0 else 16 + 128 * s
        rows = slice(top, 16 + 128 * (s + 1))
        cols = slice(16 + 128 * s, 16 + PAST)
        strip = dot_nt(hi[rows], hi[cols], None) + (dot_nt(hi[rows], lo[cols], None) + dot_nt(lo[rows], hi[cols], None))
        if s == 0:
            g = strip[0:8]
            strip = strip[16:]
            own = dot_nt(hi[0:16], hi[0:16], None) + (dot_nt(hi[0:16], lo[0:16], None) + dot_nt(lo[0:16], hi[0:16], None))
            corner = own[0:1, 0:1]
        for b in range(s, 4):
            block = strip[:, 128 * (b - s) : 128 * (b - s + 1)].reshape(16, 8, 128)
            part[at * 16 : at * 16 + 16] = block
            if b == s:
                gb = g[:, 128 * b : 128 * b + 128]
                packed = jnp.where(row == 0, gb, jnp.where(row == 1, pltpu.roll(gb, 64, 1), corner))
                part[at * 16 + 8] = jnp.where(lane < 64, packed, block[8])
            at += 1

    pl.semaphore_wait(barrier, 19)
    swap = pltpu.make_async_remote_copy(
        part.at[pl.ds((1 - c) * HALF, HALF)], recv0, s0, r0, device_id=partner, device_id_type=MESH
    )
    swap.start()
    swap.wait_recv()
    mine[...] = part[pl.ds(c * HALF, HALF)] + recv0[...]

    copies = []
    for o in range(15, 0, -1):
        copy = pltpu.make_async_remote_copy(
            mine.at[pl.ds(plane_target(o) * PIECE, PIECE)], buf_a.at[o], sa.at[o], ra.at[o], device_id=plane(o), device_id_type=MESH
        )
        copy.start()
        copies.append(copy)
    here = y * 4 + x
    total = mine[pl.ds(here * PIECE, PIECE)]
    for o in range(1, 16):
        copies[15 - o].wait_recv()
        total = total + buf_a[o]
    buf_b[z] = total
    for dz in range(1, 4):
        copy = pltpu.make_async_remote_copy(
            buf_b.at[z], buf_b.at[z], sb.at[dz], rb.at[dz], device_id={"rows_0": ring("rows_0", dz)}, device_id_type=MESH
        )
        copy.start()
        copies.append(copy)
    for dz in range(1, 4):
        copies[14 + dz].wait_recv()
    place = c * HALF + here * PIECE
    out_ref[pl.ds(place, PIECE)] = (buf_b[0] + buf_b[1]) + (buf_b[2] + buf_b[3])
    gathers = {}
    for o in range(15, 0, -1):
        copy = pltpu.make_async_remote_copy(
            out_ref.at[pl.ds(place, PIECE)],
            out_ref.at[pl.ds(place, PIECE)],
            sg.at[o],
            rg.at[o],
            device_id=plane(o),
            device_id_type=MESH,
        )
        copy.start()
        copies.append(copy)
        gathers[o] = copy
    forwards = []
    for o in range(16):
        if o:
            gathers[o].wait_recv()
        spot = pl.ds(c * HALF + plane_source(o) * PIECE, PIECE)
        copy = pltpu.make_async_remote_copy(
            out_ref.at[spot], out_ref.at[spot], sd.at[o], rd.at[o], device_id=partner, device_id_type=MESH
        )
        copy.start()
        forwards.append(copy)
    swap.wait_send()
    for copy in copies:
        copy.wait_send()
    for copy in forwards:
        copy.wait()


def gram(snapshots):
    dma = pltpu.SemaphoreType.DMA
    return pl.pallas_call(
        gram_kernel,
        out_shape=jax.ShapeDtypeStruct((TILES, 8, 128), F32),
        in_specs=[pl.BlockSpec(memory_space=pltpu.VMEM)],
        out_specs=pl.BlockSpec(memory_space=pltpu.VMEM),
        scratch_shapes=[
            pltpu.VMEM((16 + PAST, CELLS_HERE), BF16),
            pltpu.VMEM((16 + PAST, CELLS_HERE), BF16),
            pltpu.VMEM((TILES, 8, 128), F32),
            pltpu.VMEM((HALF, 8, 128), F32),
            pltpu.VMEM((HALF, 8, 128), F32),
            pltpu.VMEM((16, PIECE, 8, 128), F32),
            pltpu.VMEM((4, PIECE, 8, 128), F32),
            dma(()),
            dma(()),
            dma((16,)),
            dma((16,)),
            dma((4,)),
            dma((4,)),
            dma((16,)),
            dma((16,)),
            dma((16,)),
            dma((16,)),
        ],
        compiler_params=pltpu.CompilerParams(collective_id=0, has_side_effects=True),
        name="gram",
    )(snapshots)


def rest_kernel(tiles_ref, right_ref, x_hbm, modes_ref, operator_ref, coef_ref, gp, xv, sem, *, root):
    load = pltpu.make_async_copy(x_hbm, xv, sem)
    load.start()
    lane8 = iota((1, 128), 1)
    low_left = (iota((128, 128), 0) >= 64) & (iota((128, 128), 1) < 64)
    pieces, corner = [], None
    for n, (i, j) in enumerate(BLOCKS):
        block = tiles_ref[16 * n : 16 * n + 16].reshape(128, 128)
        if i == j:
            extra = block[64:72]
            pieces.append(jnp.where(lane8 < 64, extra[0:1], pltpu.roll(extra[1:2], 64, 1)))
            if corner is None:
                corner = extra[2:3, 0:1]
            block = jnp.where(low_left, block.T, block)
        else:
            gp[128 * j : 128 * j + 128, 128 * i : 128 * i + 128] = block.T
        gp[128 * i : 128 * i + 128, 128 * j : 128 * j + 128] = block
    g = jnp.concatenate(pieces, 1)
    first = iota((W, PAST), 1) == 0

    def products(vt):
        around = pltpu.roll(vt, 1, 1)
        shifted = jnp.where(first, 0.0, around)
        end = vt[:, PAST - 1 : PAST]
        both = dot_nn(jnp.concatenate([vt, shifted], 0), gp[...])
        q = both[W:] + end * g
        q_end = jnp.sum(shifted * g, 1, keepdims=True) + end * corner
        q_around = jnp.where(first, q_end, q)
        q_wide = jnp.concatenate([q, jnp.where(iota((W, 128), 1) == 0, q_end, 0.0)], 1)
        return both[:W], around, q_around, q_wide

    v1 = right_ref[...]
    a, v1c, q1c, q1 = products(v1)
    m1 = dot_nt(a, v1)
    c11 = dot_nt(q1c, v1c)
    e = a - dot_nn(m1, v1)
    eye = iota((W, W), 0) == iota((W, W), 1)
    e = e / jnp.sum(jnp.where(eye, m1, 0.0), 1, keepdims=True)
    f1, fc1 = eliminate([m1, c11])
    b, ec, q2c, q2 = products(e)
    h12 = dot_nt(a, e)
    h22 = dot_nt(b, e)
    c12 = dot_nt(q1c, ec)
    c22 = dot_nt(q2c, ec)
    u12 = apply_x(f1, h12)
    uc12 = apply_x(fc1, c12)
    f2, fc2 = eliminate([h22 - dot_tn(u12, u12), c22 - dot_tn(uc12, uc12)])

    w1 = apply_x(f1, jnp.concatenate([v1, v1c, q1], 1))
    y2 = jnp.concatenate([e, ec, q2], 1) - dot_tn(u12, w1)
    w2 = apply_x(f2, y2)
    wt = jnp.concatenate([w1[:, :PAST], w2[:, :PAST]], 0)
    qw = jnp.concatenate([w1[:, 2 * PAST : 3 * PAST], w2[:, 2 * PAST : 3 * PAST]], 0)
    operator_ref[...] = dot_nt(wt, qw)

    t1 = apply_x(fc1, q1)
    y_2 = apply_xt(fc2, apply_x(fc2, q2 - dot_tn(uc12, t1)))
    y_1 = apply_xt(fc1, t1 - dot_nn(uc12, y_2))
    top = apply_u(f1, y_1) + dot_nn(u12, y_2)
    coef = jnp.concatenate([top, apply_u(f2, y_2)], 0) * (1.0 / root)
    coef_ref[:, :PAST] = coef[:, :PAST]
    coef_ref[:, PAST : PAST + 1] = coef[:, PAST : PAST + 1]

    load.wait()
    xv[0:1] = xv[PAST : PAST + 1]
    wc = jnp.concatenate([w1[:, PAST : 2 * PAST], w2[:, PAST : 2 * PAST]], 0) * root
    modes_ref[...] = dot_nn(wc, xv[0:PAST], lax.Precision.HIGH)


def rest(tiles, right, snapshots, cells):
    vm = pl.BlockSpec(memory_space=pltpu.VMEM)
    order = 2 * W
    return pl.pallas_call(
        lambda *refs: rest_kernel(*refs, root=float(cells) ** 0.5),
        out_shape=[
            jax.ShapeDtypeStruct((order, CELLS_HERE), F32),
            jax.ShapeDtypeStruct((order, order), F32),
            jax.ShapeDtypeStruct((order, PAST + 1), F32),
        ],
        in_specs=[vm, vm, pl.BlockSpec(memory_space=pl.ANY)],
        out_specs=[vm, vm, vm],
        scratch_shapes=[
            pltpu.VMEM((PAST, PAST), F32),
            pltpu.VMEM((PAST + 1, CELLS_HERE), F32),
            pltpu.SemaphoreType.DMA(()),
        ],
        compiler_params=pltpu.CompilerParams(vmem_limit_bytes=40 * 1024 * 1024),
        name="rest",
    )(tiles, right, snapshots)


def orth(start):
    vm = pl.BlockSpec(memory_space=pltpu.VMEM)
    return pl.pallas_call(
        orth_kernel, out_shape=jax.ShapeDtypeStruct((W, PAST), F32), in_specs=[vm], out_specs=vm, name="orth"
    )(start)


def shards(snapshots, start):
    cells = snapshots.shape[1] * lax.axis_size(ROWS_SUB)
    right = orth(start)
    tiles = gram(snapshots)
    return tuple(rest(tiles, right, snapshots, cells))


def solution(mesh):
    finer = Mesh(mesh.devices.reshape(4, 4, 2, mesh.shape["sub"]), ROWS_SUB)
    return jax.shard_map(
        shards,
        mesh=finer,
        in_specs=(P(None, ROWS_SUB), P()),
        out_specs=(P(None, ROWS_SUB), P(), P()),
        check_vma=False,
    )
```

profile of v0, /device:TPU:1, one launch (start us, length us, event | category | flops | bytes accessed | tf_op | source)
XLA Modules:
  0.0 49.4 jit_solution(11804623067335156488)
XLA Ops:
  0.6 0.0 copy-start
  0.6 1.9 %copy.5.start_ref = f32[512,64]{1,0:T(8,128)} copy(f32[512,64]{0,1:T(8,128)} %param.3) | data formatting | bytes 262144 | tf_op args[1]
  2.5 4.1 %orth.1.refs_1_ = f32[64,512]{1,0:T(8,128)} custom-call(f32[512,64]{1,0:T(8,128)} %copy.5.start_ref), custom_call_target="tpu_custom_call" | custom-call | tf_op jit(solution)/shard_map/orth/pallas_call | solution.py:336
  6.6 0.0 copy-start.2
  6.6 30.8 %gram.1.refs_0_ = f32[160,8,128]{2,1,0:T(8,128)} custom-call(f32[513,1024]{1,0:T(8,128)} %refs_2_.1), custom_call_target="tpu_custom_call" | custom-call | tf_op jit(solution)/shard_map/gram/pallas_call | solution.py:214
  37.4 0.0 copy-done
  37.5 0.0 copy-done.2
  37.5 0.0 copy-start.1
  37.5 1.1 %copy-done.1 = f32[160,8,128]{2,1,0:T(8,128)S(1)} copy-done((f32[160,8,128]{2,1,0:T(8,128)S(1)}, f32[160,8,128]{2,1,0:T(8,128)}, u32[]{:S(2)}) %copy-start.1) | copy-done | bytes 655384
  38.6 10.0 %rest.1 = (f32[128,1024]{1,0:T(8,128)}, f32[128,128]{1,0:T(8,128)}, f32[128,513]{1,0:T(8,128)S(1)}) custom-call(f32[160,8,128]{2,1,0:T(8,128)S(1)} %copy-done.1, f32[64,512]{1,0:T(8,128)S(1)} %copy-done.2, f32[513,1024]{1,0:T(8,128)S(1)} %copy-done), custom_call_target="tpu_custom_call" | custom-call | tf_op jit(solution)/shard_map/rest/pallas_call | solution.py:315
  48.5 0.8 %copy.6 = f32[128,513]{0,1:T(8,128)} copy(f32[128,513]{1,0:T(8,128)S(1)} %get-tuple-element.5) | data formatting | bytes 525312 | tf_op jit(solution)/shard_map/rest/pallas_call | solution.py:315
Async XLA Ops:
  0.6 36.8 %copy-start = (f32[513,1024]{1,0:T(8,128)S(1)}, f32[513,1024]{1,0:T(8,128)}, u32[]{:S(2)}) copy-start(f32[513,1024]{1,0:T(8,128)} %refs_2_.1) | copy-start | bytes 6303748
  6.6 30.9 %copy-start.2 = (f32[64,512]{1,0:T(8,128)S(1)}, f32[64,512]{1,0:T(8,128)}, u32[]{:S(2)}) copy-start(f32[64,512]{1,0:T(8,128)} %orth.1.refs_1_) | copy-start | bytes 393220
  37.5 1.1 %copy-start.1 = (f32[160,8,128]{2,1,0:T(8,128)S(1)}, f32[160,8,128]{2,1,0:T(8,128)}, u32[]{:S(2)}) copy-start(f32[160,8,128]{2,1,0:T(8,128)} %gram.1.refs_0_) | copy-start | bytes 1966084
where the time goes:
time: 49.6 us; the launch traced here: 49.4 us
  Pallas kernels  44.9 us (91%)
  local copies, waits for them, and re-layouts  3.82 us (8%)
  between operations  0.68 us (1%)
    pallas_call x1, Pallas kernels, gram(): pl.pallas_call(gram_kernel, out_shape=jax.ShapeDtypeStruct((TILES, 8, 128...  30.8 us
    pallas_call x1, Pallas kernels, rest(): pl.pallas_call(lambda *refs: rest_kernel(*refs, root=float(cells) ** 0.5)...  9.96 us
    pallas_call x1, Pallas kernels, orth(): pl.pallas_call(orth_kernel, out_shape=jax.ShapeDtypeStruct((W, PAST), F32...  4.06 us
    unnamed x7, local copies, waits for them, and re-layouts  2.98 us

commit v1 on v0

--- a/solution.py
+++ b/solution.py
@@ -14,10 +14,13 @@
 W = 64
 PAST = 512
 CELLS_HERE = 1024
-BLOCKS = [(0, 0), (0, 1), (0, 2), (0, 3), (1, 1), (1, 2), (1, 3), (2, 2), (2, 3), (3, 3)]
+BLOCKS = [(0, 0), (0, 1), (0, 2), (2, 2), (2, 3)] + [(1, 1), (1, 2), (1, 3), (3, 3), (3, 0)]
 TILES = 16 * len(BLOCKS)
 HALF = TILES // 2
 PIECE = HALF // 16
+CHUNKS = 2
+DEPTH = CELLS_HERE // CHUNKS
+GRANT = 24
 
 
 def dot_nn(a, b, precision=HI):
@@ -83,11 +86,8 @@
     return dot_tn(fac, z)[W:]
 
 
-def orth_kernel(start_ref, out_ref):
-    start = start_ref[...]
-    st = jnp.concatenate([start, jnp.zeros_like(start)], 1).T[:W]
-    fac = eliminate([dot_nt(st, st)])[0]
-    out_ref[...] = apply_x(fac, st)
+def orth_rows(st):
+    return apply_x(eliminate([dot_nt(st, st)])[0], st)
 
 
 def ring(axis, step):
@@ -95,9 +95,20 @@
     return lax.rem(lax.axis_index(axis) + (step + n) % n, n)
 
 
-def gram_kernel(x_ref, out_ref, hi, lo, part, mine, recv0, buf_a, buf_b, s0, r0, sa, ra, sb, rb, sg, rg, sd, rd):
+def gram_kernel(
+    x_hbm, start_hbm, out_ref, right_ref, xv, sv, hi, lo, hx, lx, part, mine, recv0, buf_a, buf_b, sx, ss, s0, r0, sa, ra, sb, rb, sg, rg, sd, rd
+):
+    loads = []
+    for t in range(CHUNKS):
+        cols = pl.ds(t * DEPTH, DEPTH)
+        loads.append(pltpu.make_async_copy(x_hbm.at[:, cols], xv.at[:, cols], sx.at[t]))
+        loads[-1].start()
+    start_load = pltpu.make_async_copy(start_hbm, sv, ss)
+    start_load.start()
     z, y, c, x = (lax.axis_index(a) for a in ROWS_SUB)
     offsets = [(o // 4, o % 4) for o in range(16)]
+    hops = [min(dy, 4 - dy) + min(dx, 4 - dx) for dy, dx in offsets]
+    near_first = sorted(range(1, 16), key=lambda o: hops[o])
 
     def plane(o):
         return {"rows_1": ring("rows_1", offsets[o][0]), "sub": ring("sub", offsets[o][1])}
@@ -110,63 +121,80 @@
 
     barrier = pltpu.get_barrier_semaphore()
     partner = {"rows_2": 1 - c}
-    pl.semaphore_signal(barrier, inc=1, device_id=partner, device_id_type=MESH)
-    for o in range(1, 16):
+    for o in near_first[::-1]:
         pl.semaphore_signal(barrier, inc=1, device_id=plane(o), device_id_type=MESH)
     for dz in range(1, 4):
         pl.semaphore_signal(barrier, inc=1, device_id={"rows_0": ring("rows_0", dz)}, device_id_type=MESH)
-
-    last = jnp.broadcast_to(x_ref[PAST : PAST + 1], (16, CELLS_HERE))
-    hl = last.astype(BF16)
-    hi[0:16] = hl
-    lo[0:16] = (last - hl.astype(F32)).astype(BF16)
-    for r in range(0, PAST, 128):
-        v = x_ref[r : r + 128]
-        h = v.astype(BF16)
-        hi[16 + r : 144 + r] = h
-        lo[16 + r : 144 + r] = (v - h.astype(F32)).astype(BF16)
+    pl.semaphore_signal(barrier, inc=1, device_id=partner, device_id_type=MESH)
+
     lane = iota((8, 128), 1)
     row = iota((8, 128), 0)
-    at = 0
-    g = None
-    for s in range(4):
-        top = 0 if s == 0 else 16 + 128 * s
-        rows = slice(top, 16 + 128 * (s + 1))
-        cols = slice(16 + 128 * s, 16 + PAST)
-        strip = dot_nt(hi[rows], hi[cols], None) + (dot_nt(hi[rows], lo[cols], None) + dot_nt(lo[rows], hi[cols], None))
-        if s == 0:
-            g = strip[0:8]
-            strip = strip[16:]
-            own = dot_nt(hi[0:16], hi[0:16], None) + (dot_nt(hi[0:16], lo[0:16], None) + dot_nt(lo[0:16], hi[0:16], None))
-            corner = own[0:1, 0:1]
-        for b in range(s, 4):
-            block = strip[:, 128 * (b - s) : 128 * (b - s + 1)].reshape(16, 8, 128)
-            part[at * 16 : at * 16 + 16] = block
-            if b == s:
-                gb = g[:, 128 * b : 128 * b + 128]
-                packed = jnp.where(row == 0, gb, jnp.where(row == 1, pltpu.roll(gb, 64, 1), corner))
-                part[at * 16 + 8] = jnp.where(lane < 64, packed, block[8])
-            at += 1
-
-    pl.semaphore_wait(barrier, 19)
+    own_g = {}
+    corner = jnp.zeros((1, 1), F32)
     swap = pltpu.make_async_remote_copy(
         part.at[pl.ds((1 - c) * HALF, HALF)], recv0, s0, r0, device_id=partner, device_id_type=MESH
     )
-    swap.start()
+    for t in range(CHUNKS):
+        k = slice(t * DEPTH, (t + 1) * DEPTH)
+        loads[t].wait()
+        last = xv[PAST : PAST + 1, k]
+        corner = corner + jnp.sum(last * last, 1, keepdims=True)
+        last = jnp.broadcast_to(last, (16, DEPTH))
+        hl = last.astype(BF16)
+        hx[:, k] = hl
+        lx[:, k] = (last - hl.astype(F32)).astype(BF16)
+        for r in range(0, PAST, 128):
+            v = xv[r : r + 128, k]
+            h = v.astype(BF16)
+            low = (v - h.astype(F32)).astype(BF16)
+            hi[r : r + 128, k] = h
+            lo[r : r + 128, k] = low
+            if r == 0:
+                hi[PAST : PAST + 128, k] = h
+                lo[PAST : PAST + 128, k] = low
+        for own in range(2):
+            p = c if own else 1 - c
+            for s in range(2):
+                first = pl.multiple_of((p + 2 * s) * 128, 128)
+                width = 384 - 128 * s
+                lines, across = pl.ds(first, 128), pl.ds(first, width)
+                a = jnp.concatenate([hx[:, k], hi[lines, k]], 0)
+                b = jnp.concatenate([lx[:, k], lo[lines, k]], 0)
+                strip = dot_nt(a, hi[across, k], None) + (dot_nt(a, lo[across, k], None) + dot_nt(b, hi[across, k], None))
+                gs = strip[0:8, 0:128]
+                if t:
+                    gs = gs + own_g[own, s]
+                own_g[own, s] = gs
+                for n in range(width // 128):
+                    spot = p * HALF + 16 * (3 * s + n)
+                    block = strip[16:, 128 * n : 128 * n + 128].reshape(16, 8, 128)
+                    if t:
+                        block = block + part[pl.ds(spot, 16)]
+                    part[pl.ds(spot, 16)] = block
+                    if n == 0 and t == CHUNKS - 1:
+                        packed = jnp.where(row == 0, gs, jnp.where(row == 1, pltpu.roll(gs, 64, 1), corner))
+                        part[spot + 8] = jnp.where(lane < 64, packed, block[8])
+            if t == CHUNKS - 1 and own == 0:
+                pl.semaphore_wait(barrier, 19)
+                swap.start()
+
     swap.wait_recv()
     mine[...] = part[pl.ds(c * HALF, HALF)] + recv0[...]
 
     copies = []
-    for o in range(15, 0, -1):
-        copy = pltpu.make_async_remote_copy(
+    arrivals = {}
+    for o in near_first[::-1]:
+        arrivals[o] = pltpu.make_async_remote_copy(
             mine.at[pl.ds(plane_target(o) * PIECE, PIECE)], buf_a.at[o], sa.at[o], ra.at[o], device_id=plane(o), device_id_type=MESH
         )
-        copy.start()
-        copies.append(copy)
+        arrivals[o].start()
+        copies.append(arrivals[o])
+    start_load.wait()
+    right_ref[...] = orth_rows(sv[...])
     here = y * 4 + x
     total = mine[pl.ds(here * PIECE, PIECE)]
-    for o in range(1, 16):
-        copies[15 - o].wait_recv()
+    for o in near_first:
+        arrivals[o].wait_recv()
         total = total + buf_a[o]
     buf_b[z] = total
     for dz in range(1, 4):
@@ -175,25 +203,20 @@
         )
         copy.start()
         copies.append(copy)
-    for dz in range(1, 4):
-        copies[14 + dz].wait_recv()
+    for copy in copies[-3:]:
+        copy.wait_recv()
     place = c * HALF + here * PIECE
     out_ref[pl.ds(place, PIECE)] = (buf_b[0] + buf_b[1]) + (buf_b[2] + buf_b[3])
     gathers = {}
-    for o in range(15, 0, -1):
-        copy = pltpu.make_async_remote_copy(
-            out_ref.at[pl.ds(place, PIECE)],
-            out_ref.at[pl.ds(place, PIECE)],
-            sg.at[o],
-            rg.at[o],
-            device_id=plane(o),
-            device_id_type=MESH,
+    for o in near_first[::-1]:
+        spot = pl.ds(place, PIECE)
+        gathers[o] = pltpu.make_async_remote_copy(
+            out_ref.at[spot], out_ref.at[spot], sg.at[o], rg.at[o], device_id=plane(o), device_id_type=MESH
         )
-        copy.start()
-        copies.append(copy)
-        gathers[o] = copy
+        gathers[o].start()
+        copies.append(gathers[o])
     forwards = []
-    for o in range(16):
+    for o in [0] + near_first:
         if o:
             gathers[o].wait_recv()
         spot = pl.ds(c * HALF + plane_source(o) * PIECE, PIECE)
@@ -209,23 +232,30 @@
         copy.wait()
 
 
-def gram(snapshots):
+def gram(snapshots, start_rows):
     dma = pltpu.SemaphoreType.DMA
+    vm = pl.BlockSpec(memory_space=pltpu.VMEM)
     return pl.pallas_call(
         gram_kernel,
-        out_shape=jax.ShapeDtypeStruct((TILES, 8, 128), F32),
-        in_specs=[pl.BlockSpec(memory_space=pltpu.VMEM)],
-        out_specs=pl.BlockSpec(memory_space=pltpu.VMEM),
+        out_shape=[jax.ShapeDtypeStruct((TILES, 8, 128), F32), jax.ShapeDtypeStruct((W, PAST), F32)],
+        in_specs=[pl.BlockSpec(memory_space=pltpu.HBM)] * 2,
+        out_specs=[vm, vm],
         scratch_shapes=[
-            pltpu.VMEM((16 + PAST, CELLS_HERE), BF16),
-            pltpu.VMEM((16 + PAST, CELLS_HERE), BF16),
+            pltpu.VMEM((PAST + 1, CELLS_HERE), F32),
+            pltpu.VMEM((W, PAST), F32),
+            pltpu.VMEM((PAST + 128, CELLS_HERE), BF16),
+            pltpu.VMEM((PAST + 128, CELLS_HERE), BF16),
+            pltpu.VMEM((16, CELLS_HERE), BF16),
+            pltpu.VMEM((16, CELLS_HERE), BF16),
             pltpu.VMEM((TILES, 8, 128), F32),
             pltpu.VMEM((HALF, 8, 128), F32),
             pltpu.VMEM((HALF, 8, 128), F32),
             pltpu.VMEM((16, PIECE, 8, 128), F32),
             pltpu.VMEM((4, PIECE, 8, 128), F32),
+            dma((CHUNKS,)),
             dma(()),
             dma(()),
+            dma(()),
             dma((16,)),
             dma((16,)),
             dma((4,)),
@@ -235,9 +265,11 @@
             dma((16,)),
             dma((16,)),
         ],
-        compiler_params=pltpu.CompilerParams(collective_id=0, has_side_effects=True),
+        compiler_params=pltpu.CompilerParams(
+            collective_id=0, has_side_effects=True, vmem_limit_bytes=GRANT * 1024 * 1024
+        ),
         name="gram",
-    )(snapshots)
+    )(snapshots, start_rows)
 
 
 def rest_kernel(tiles_ref, right_ref, x_hbm, modes_ref, operator_ref, coef_ref, gp, xv, sem, *, root):
@@ -245,19 +277,19 @@
     load.start()
     lane8 = iota((1, 128), 1)
     low_left = (iota((128, 128), 0) >= 64) & (iota((128, 128), 1) < 64)
-    pieces, corner = [], None
+    pieces, corner = {}, None
     for n, (i, j) in enumerate(BLOCKS):
         block = tiles_ref[16 * n : 16 * n + 16].reshape(128, 128)
         if i == j:
             extra = block[64:72]
-            pieces.append(jnp.where(lane8 < 64, extra[0:1], pltpu.roll(extra[1:2], 64, 1)))
+            pieces[i] = jnp.where(lane8 < 64, extra[0:1], pltpu.roll(extra[1:2], 64, 1))
             if corner is None:
                 corner = extra[2:3, 0:1]
             block = jnp.where(low_left, block.T, block)
         else:
             gp[128 * j : 128 * j + 128, 128 * i : 128 * i + 128] = block.T
         gp[128 * i : 128 * i + 128, 128 * j : 128 * j + 128] = block
-    g = jnp.concatenate(pieces, 1)
+    g = jnp.concatenate([pieces[i] for i in range(4)], 1)
     first = iota((W, PAST), 1) == 0
 
     def products(vt):
@@ -300,8 +332,7 @@
     y_1 = apply_xt(fc1, t1 - dot_nn(uc12, y_2))
     top = apply_u(f1, y_1) + dot_nn(u12, y_2)
     coef = jnp.concatenate([top, apply_u(f2, y_2)], 0) * (1.0 / root)
-    coef_ref[:, :PAST] = coef[:, :PAST]
-    coef_ref[:, PAST : PAST + 1] = coef[:, PAST : PAST + 1]
+    coef_ref[...] = coef.T[: PAST + 1]
 
     load.wait()
     xv[0:1] = xv[PAST : PAST + 1]
@@ -317,32 +348,26 @@
         out_shape=[
             jax.ShapeDtypeStruct((order, CELLS_HERE), F32),
             jax.ShapeDtypeStruct((order, order), F32),
-            jax.ShapeDtypeStruct((order, PAST + 1), F32),
+            jax.ShapeDtypeStruct((PAST + 1, order), F32),
         ],
-        in_specs=[vm, vm, pl.BlockSpec(memory_space=pl.ANY)],
+        in_specs=[vm, vm, pl.BlockSpec(memory_space=pltpu.HBM)],
         out_specs=[vm, vm, vm],
         scratch_shapes=[
             pltpu.VMEM((PAST, PAST), F32),
             pltpu.VMEM((PAST + 1, CELLS_HERE), F32),
             pltpu.SemaphoreType.DMA(()),
         ],
-        compiler_params=pltpu.CompilerParams(vmem_limit_bytes=40 * 1024 * 1024),
+        compiler_params=pltpu.CompilerParams(vmem_limit_bytes=GRANT * 1024 * 1024),
         name="rest",
     )(tiles, right, snapshots)
 
 
-def orth(start):
-    vm = pl.BlockSpec(memory_space=pltpu.VMEM)
-    return pl.pallas_call(
-        orth_kernel, out_shape=jax.ShapeDtypeStruct((W, PAST), F32), in_specs=[vm], out_specs=vm, name="orth"
-    )(start)
-
-
 def shards(snapshots, start):
     cells = snapshots.shape[1] * lax.axis_size(ROWS_SUB)
-    right = orth(start)
-    tiles = gram(snapshots)
-    return tuple(rest(tiles, right, snapshots, cells))
+    snapshots = pltpu.with_memory_space_constraint(snapshots, pltpu.HBM)
+    tiles, right = gram(snapshots, pltpu.with_memory_space_constraint(start.T, pltpu.HBM))
+    modes, operator, coef = rest(tiles, right, snapshots, cells)
+    return modes, operator, coef.T
 
 
 def solution(mesh):

time: 49.6 us -> 39.8 us (0.80)
  Pallas kernels: 44.9 us -> 39 us
  local copies, waits for them, and re-layouts: 3.82 us -> 0 us
    pallas_call x2 -> x1, Pallas kernels: 34.9 us -> 29.2 us  [gram(): pl.pallas_call(gram_kernel, out_shape=[jax.ShapeDtypeStruct((TILES, 8, 12...]
    unnamed x7 -> x0, local copies, waits for them, and re-layouts: 2.98 us -> none
    pallas_call x1 -> x0, local copies, waits for them, and re-layouts: 0.84 us -> none  [rest(): pl.pallas_call(lambda *refs: rest_kernel(*refs, root=float(cells) ** 0.5)...]
where the time goes in v1:
time: 39.8 us; the launch traced here: 39.7 us
  Pallas kernels  39 us (98%)
  between operations  0.64 us (2%)
    pallas_call x1, Pallas kernels, gram(): pl.pallas_call(gram_kernel, out_shape=[jax.ShapeDtypeStruct((TILES, 8, 12...  29.2 us
    pallas_call x1, Pallas kernels, rest(): pl.pallas_call(lambda *refs: rest_kernel(*refs, root=float(cells) ** 0.5)...  9.83 us

profile of v1, /device:TPU:1, one launch (start us, length us, event | category | flops | bytes accessed | tf_op | source)
XLA Modules:
  0.0 39.7 jit_solution(4803603421370199964)
XLA Ops:
  0.6 29.2 %gram.1 = (f32[160,8,128]{2,1,0:T(8,128)S(1)}, f32[64,512]{1,0:T(8,128)S(1)}) custom-call(f32[513,1024]{1,0:T(8,128)} %refs_2_.1, f32[64,512]{1,0:T(8,128)} %bitcast.2), custom_call_target="tpu_custom_call" | custom-call | tf_op jit(solution)/shard_map/gram/pallas_call | solution.py:238
  29.8 9.8 %rest.1 = (f32[128,1024]{1,0:T(8,128)}, f32[128,128]{1,0:T(8,128)}, f32[513,128]{1,0:T(8,128)}) custom-call(f32[160,8,128]{2,1,0:T(8,128)S(1)} %get-tuple-element.8.refs_0_, f32[64,512]{1,0:T(8,128)S(1)} %get-tuple-element.9.refs_1_, f32[513,1024]{1,0:T(8,128)} %refs_2_.1), custom_call_target="tpu_custom_call" | custom-call | tf_op jit(solution)/shard_map/rest/pallas_call | solution.py:346
